TPU v7x, 32 devices: a whole 2x2x4 slice. The times are simulated.
32 devices in a mesh: gx: 8 (over y, x, core), gy: 4 (over z).
Axes of the slice: x: 2, y: 2, z: 4, core: 2. Of those that a mesh axis runs over, the one named last changes fastest.
Arguments:
- collocation: bfloat16 [3072, 16384], P(None, 'gx'), may hold values from -6 to 6
- density: bfloat16 [3072, 3072], P('gy'), may hold values from -0.109375 to 0.109375
- kernel: bfloat16 [16384, 8, 4, 512], P('gx', None, 'gy'), may hold values from -6.67572e-06 to 6.67572e-06
Outputs:
- exchange: float32 [3072, 3072], P('gx', 'gy')
All inputs are finite; a program needn't handle non-finite values.
Results may differ from a plain program's by a relative error of at most 0.008.
Values may be sent and summed in bfloat16 or wider, within the bound.
A program may use at most 448 MiB of HBM per device.

v0:
```python
import jax
import jax.numpy as jnp
from jax import lax
from jax.sharding import PartitionSpec as P

F32 = jnp.float32
BF16 = jnp.bfloat16


def spread(block, axis_size, axis):
    rows = block.shape[0]
    me = lax.axis_index("gy")
    out = jnp.zeros((axis_size * rows, block.shape[1]), block.dtype)
    out = lax.dynamic_update_slice_in_dim(out, block, me * rows, 0)
    for shift in range(1, axis_size):
        pairs = [(k, (k + shift) % axis_size) for k in range(axis_size)]
        got = lax.ppermute(block, axis, pairs)
        source = lax.rem(me + axis_size - shift, axis_size)
        out = lax.dynamic_update_slice_in_dim(out, got, source * rows, 0)
    return out


def exchange_sum(part, axis_size, axis):
    width = part.shape[1] // axis_size
    me = lax.axis_index(axis)
    total = lax.dynamic_slice_in_dim(part, me * width, width, 1).astype(F32)
    for shift in range(1, axis_size):
        pairs = [(k, (k + shift) % axis_size) for k in range(axis_size)]
        target = lax.rem(me + shift, axis_size)
        sent = lax.dynamic_slice_in_dim(part, target * width, width, 1)
        total = total + lax.ppermute(sent, axis, pairs).astype(F32)
    return total


def build(n_gx, n_gy):
    def local(collocation, density, kernel):
        nbf, panel_rows = collocation.shape
        piece = kernel.shape[3]
        i, j = lax.axis_index("gx"), lax.axis_index("gy")
        halves = 2 if piece % 256 == 0 else 1
        half = piece // halves
        own = [
            lax.dynamic_slice_in_dim(collocation, j * piece + h * half, half, 1)
            for h in range(halves)
        ]
        gathered = [lax.all_gather(own[0], "gx", axis=1, tiled=True)]

        cols = nbf // n_gx
        strip = spread(lax.dynamic_slice_in_dim(density, i * cols, cols, 1), n_gy, "gy")
        whole = lax.all_gather(strip, "gx", axis=0, tiled=False)
        for h in range(1, halves):
            later, whole = lax.optimization_barrier((own[h], whole))
            gathered.append(lax.all_gather(later, "gx", axis=1, tiled=True))
        dense = lax.dot_general(
            whole,
            collocation.reshape(n_gx, cols, panel_rows),
            (((0, 2), (0, 1)), ((), ())),
            preferred_element_type=F32,
        ).astype(BF16)

        weighted = []
        for h in range(halves):
            tile = kernel[:, :, 0, h * half : (h + 1) * half].reshape(panel_rows, -1)
            products = lax.dot_general(
                dense, gathered[h], (((0,), (0,)), ((), ())), preferred_element_type=F32
            )
            weighted.append((tile.astype(F32) * products).astype(BF16))

        parts = 3 if (nbf // n_gy) % 384 == 0 else 1
        sub = nbf // n_gy // parts
        done = []
        for c in range(parts):
            contracted = 0.0
            for h in range(halves):
                rows = gathered[h].reshape(n_gy, parts, sub, -1)[:, c].reshape(n_gy * sub, -1)
                contracted = contracted + lax.dot_general(
                    rows, weighted[h], (((1,), (1,)), ((), ())), preferred_element_type=F32
                )
            term = lax.dot_general(
                collocation,
                contracted.astype(BF16),
                (((1,), (1,)), ((), ())),
                preferred_element_type=F32,
            ).astype(BF16)
            summed = lax.psum_scatter(term, "gx", scatter_dimension=0, tiled=True)
            done.append(exchange_sum(summed, n_gy, "gy"))
        return jnp.concatenate(done, axis=1)

    return local


def solution(mesh):
    return jax.shard_map(
        build(mesh.shape["gx"], mesh.shape["gy"]),
        mesh=mesh,
        in_specs=(P(None, "gx"), P("gy", None), P("gx", None, "gy", None)),
        out_specs=P("gx", "gy"),
        check_vma=False,
    )
```

profile of v0, /device:TPU:18, one launch (start us, length us, event | category | flops | bytes accessed | tf_op | source)
XLA Modules:
  0.0 605.1 jit_solution(4618804121003561843)
XLA Ops:
  6.5 3.8 constant_dynamic-slice_fusion.13
  10.4 0.2 all_gather.21
  10.6 1.2 bitcast_dynamic-update-slice_fusion.3
  11.9 1.6 collective-permute-start
  13.5 0.3 collective-permute-start.1
  13.8 1.3 collective-permute-start.2
  15.2 38.3 %collective-permute-done = bf16[768,384]{1,0:T(8,128)(2,1)} collective-permute-done((bf16[768,384]{1,0:T(8,128)(2,1)S(1)}, bf16[768,384]{1,0:T(8,128)(2,1)}, u32[]{:S(2)}, u32[]{:S(2)}) %collective-permute-start) | collective-permute-done | bytes 589856 | tf_op jit(solution)/shard_map/ppermute | solution.py:17
  53.5 1.2 bitcast_dynamic-update-slice_fusion.2
  54.7 1.2 bitcast_dynamic-update-slice_fusion.1
  55.8 7.9 %collective-permute-done.2 = bf16[768,384]{1,0:T(8,128)(2,1)S(1)} collective-permute-done((bf16[768,384]{1,0:T(8,128)(2,1)S(1)}, bf16[768,384]{1,0:T(8,128)(2,1)S(1)}, u32[]{:S(2)}, u32[]{:S(2)}) %collective-permute-start.2) | collective-permute-done | bytes 589856 | tf_op jit(solution)/shard_map/ppermute | solution.py:17
  63.8 0.1 bitcast_dynamic-update-slice_fusion
  63.9 1.4 copy-done.2
  65.4 12.4 %slice_convert_fusion = (f32[2048,8,1,256]{3,1,2,0:T(8,128)}, f32[2048,8,1,256]{3,1,2,0:T(8,128)S(1)}) fusion(bf16[2048,8,1,512]{3,1,2,0:T(8,128)(2,1)} %param.5), kind=kLoop, calls=%fused_computation.6 | loop fusion | flops 8388608 | bytes 50331648 | tf_op jit(solution)/shard_map/convert_element_type | solution.py:67
  77.7 16.0 %copy.25 = f32[256,8,8,256]{3,1,2,0:T(8,128)} copy(f32[256,8,8,256]{3,2,1,0:T(8,128)} %bitcast.73) | data formatting | bytes 33554432
  93.7 11.2 %copy.24 = f32[256,8,8,256]{3,1,2,0:T(8,128)} copy(f32[256,8,8,256]{3,2,1,0:T(8,128)S(1)} %bitcast.72) | data formatting | bytes 33554432
  104.9 8.9 %fusion.7 = (bf16[4,1,256,2048]{3,2,1,0:T(8,128)(2,1)}, bf16[4,1,256,2048]{3,2,1,0:T(8,128)(2,1)}, bf16[4,1,256,2048]{3,2,1,0:T(8,128)(2,1)}) fusion(bf16[4,3,256,2048]{3,2,1,0:T(8,128)(2,1)} %bitcast.76), kind=kLoop, calls=%fused_computation.38 | loop fusion | bytes 25165824 | tf_op jit(solution)/shard_map/slice | solution.py:75
  113.8 72.7 %all-gather.6.cloned.1.call-done = bf16[8,3072,384]{2,1,0:T(8,128)(2,1)} async-done(((bf16[1,3072,384]{2,1,0:T(8,128)(2,1)}), bf16[8,3072,384]{2,1,0:T(8,128)(2,1)}) %all-gather.6.cloned.1.call-update) | async-done | bytes 18874384 | tf_op jit(solution)/shard_map/all_gather | solution.py:50
  186.6 0.2 reduce-scatter.10.cloned.1.call-start
  186.8 46.2 %bitcast_convert_fusion = bf16[3072,2048]{1,0:T(8,128)(2,1)} fusion(bf16[8,3072,384]{2,1,0:T(8,128)(2,1)} %all-gather.6.cloned.1.call-done, bf16[8,384,2048]{2,1,0:T(8,128)(2,1)} %bitcast.84), kind=kOutput, calls=%fused_computation | convolution fusion | flops 38660997120 | bytes 44040192 | tf_op jit(solution)/shard_map/dot_general | solution.py:54
  232.9 34.7 %multiply_convert_fusion.1 = bf16[2048,2048]{1,0:T(8,128)(2,1)} fusion(f32[2048,2048]{1,0:T(8,128)S(1)} %bitcast.75, bf16[3072,2048]{1,0:T(8,128)(2,1)} %bitcast_convert_fusion, bf16[3072,2048]{1,0:T(8,128)(2,1)} %all-gather.4.cloned.1.call-done), kind=kOutput, calls=%fused_computation.2 | convolution fusion | flops 25778192384 | bytes 50331648 | tf_op jit(solution)/shard_map/dot_general | solution.py:64
  267.6 14.7 %fusion.8 = f32[1024,2048]{1,0:T(8,128)} fusion(bf16[1024,2048]{1,0:T(8,128)(2,1)} %bitcast.82, bf16[2048,2048]{1,0:T(8,128)(2,1)} %multiply_convert_fusion.1), kind=kOutput, calls=%fused_computation.39 | convolution fusion | flops 8589934592 | bytes 20971520 | tf_op jit(solution)/shard_map/dot_general | solution.py:76
  282.3 8.1 %fusion.6 = (bf16[4,1,256,2048]{3,2,1,0:T(8,128)(2,1)S(1)}, bf16[4,1,256,2048]{3,2,1,0:T(8,128)(2,1)}, bf16[4,1,256,2048]{3,2,1,0:T(8,128)(2,1)}) fusion(bf16[4,3,256,2048]{3,2,1,0:T(8,128)(2,1)} %bitcast.77), kind=kLoop, calls=%fused_computation.37 | loop fusion | bytes 25165824 | tf_op jit(solution)/shard_map/slice | solution.py:75
  290.4 3.1 copy-done.1
  293.5 33.1 %multiply_convert_fusion = bf16[2048,2048]{1,0:T(8,128)(2,1)} fusion(f32[2048,2048]{1,0:T(8,128)} %bitcast.74, bf16[3072,2048]{1,0:T(8,128)(2,1)} %bitcast_convert_fusion, bf16[3072,2048]{1,0:T(8,128)(2,1)S(1)} %copy-done.1), kind=kOutput, calls=%fused_computation.1 | convolution fusion | flops 25778192384 | bytes 50331648 | tf_op jit(solution)/shard_map/dot_general | solution.py:64
  326.6 13.2 %add_convert_fusion.10 = bf16[1024,2048]{1,0:T(8,128)(2,1)S(1)} fusion(f32[1024,2048]{1,0:T(8,128)} %fusion.8, bf16[1024,2048]{1,0:T(8,128)(2,1)S(1)} %bitcast.83, bf16[2048,2048]{1,0:T(8,128)(2,1)} %multiply_convert_fusion), kind=kOutput, calls=%fused_computation.5.clone.clone | convolution fusion | flops 8594128896 | bytes 25165824 | tf_op jit(solution)/shard_map/dot_general | solution.py:76
  339.8 17.5 %convert_bitcast_fusion.2 = bf16[3072,1024]{0,1:T(8,128)(2,1)} fusion(bf16[3072,2048]{1,0:T(8,128)(2,1)} %param.3, bf16[1024,2048]{1,0:T(8,128)(2,1)S(1)} %add_convert_fusion.10), kind=kOutput, calls=%fused_computation.10 | convolution fusion | flops 12888047616 | bytes 23068672 | tf_op jit(solution)/shard_map/dot_general | solution.py:79
  357.2 8.6 %copy.6 = bf16[3072,1024]{1,0:T(8,128)(2,1)} copy(bf16[3072,1024]{0,1:T(8,128)(2,1)} %convert_bitcast_fusion.2) | data formatting | bytes 12582912
  365.9 14.8 %fusion.9 = f32[1024,2048]{1,0:T(8,128)} fusion(bf16[1024,2048]{1,0:T(8,128)(2,1)} %bitcast.79, bf16[2048,2048]{1,0:T(8,128)(2,1)} %multiply_convert_fusion.1), kind=kOutput, calls=%fused_computation.40 | convolution fusion | flops 8589934592 | bytes 20971520 | tf_op jit(solution)/shard_map/dot_general | solution.py:76
  380.7 15.3 %add_convert_fusion.9 = bf16[1024,2048]{1,0:T(8,128)(2,1)} fusion(f32[1024,2048]{1,0:T(8,128)} %fusion.9, bf16[1024,2048]{1,0:T(8,128)(2,1)S(1)} %bitcast.81, bf16[2048,2048]{1,0:T(8,128)(2,1)} %multiply_convert_fusion), kind=kOutput, calls=%fused_computation.4.clone.clone | convolution fusion | flops 8594128896 | bytes 25165824 | tf_op jit(solution)/shard_map/dot_general | solution.py:76
  396.1 16.7 %convert_bitcast_fusion.1 = bf16[3072,1024]{0,1:T(8,128)(2,1)} fusion(bf16[3072,2048]{1,0:T(8,128)(2,1)S(1)} %bitcast.86, bf16[1024,2048]{1,0:T(8,128)(2,1)} %add_convert_fusion.9), kind=kOutput, calls=%fused_computation.9 | convolution fusion | flops 12888047616 | bytes 23068672 | tf_op jit(solution)/shard_map/dot_general | solution.py:79
  412.8 8.7 %copy.8 = bf16[3072,1024]{1,0:T(8,128)(2,1)} copy(bf16[3072,1024]{0,1:T(8,128)(2,1)} %convert_bitcast_fusion.1) | data formatting | bytes 12582912
  421.6 14.9 %fusion.10 = f32[1024,2048]{1,0:T(8,128)} fusion(bf16[1024,2048]{1,0:T(8,128)(2,1)} %bitcast.78, bf16[2048,2048]{1,0:T(8,128)(2,1)} %multiply_convert_fusion.1), kind=kOutput, calls=%fused_computation.41 | convolution fusion | flops 8589934592 | bytes 20971520 | tf_op jit(solution)/shard_map/dot_general | solution.py:76
  436.5 16.2 %add_convert_fusion.8 = bf16[1024,2048]{1,0:T(8,128)(2,1)} fusion(f32[1024,2048]{1,0:T(8,128)} %fusion.10, bf16[1024,2048]{1,0:T(8,128)(2,1)S(1)} %bitcast.80, bf16[2048,2048]{1,0:T(8,128)(2,1)} %multiply_convert_fusion), kind=kOutput, calls=%fused_computation.3.clone.clone.1 | convolution fusion | flops 8594128896 | bytes 25165824 | tf_op jit(solution)/shard_map/dot_general | solution.py:76
  452.7 16.7 %convert_bitcast_fusion = bf16[3072,1024]{0,1:T(8,128)(2,1)} fusion(bf16[3072,2048]{1,0:T(8,128)(2,1)S(1)} %bitcast.88, bf16[1024,2048]{1,0:T(8,128)(2,1)} %add_convert_fusion.8), kind=kOutput, calls=%fused_computation.8 | convolution fusion | flops 12888047616 | bytes 23068672 | tf_op jit(solution)/shard_map/dot_general | solution.py:79
  469.4 8.6 %copy.10 = bf16[3072,1024]{1,0:T(8,128)(2,1)} copy(bf16[3072,1024]{0,1:T(8,128)(2,1)} %convert_bitcast_fusion) | data formatting | bytes 12582912
  478.1 1.3 constant_dynamic-slice_fusion.11
  479.4 0.2 copy.13
  479.6 1.5 collective-permute-start.3
  481.1 0.2 copy.14
  481.3 0.6 collective-permute-start.4
  481.9 0.2 copy.15
  482.0 1.5 collective-permute-start.5
  483.5 0.2 copy.12
  483.7 9.1 %reduce-scatter.12.cloned.1.call-done = bf16[384,1024]{1,0:T(8,128)(2,1)} async-done(((bf16[3072,1024]{1,0:T(8,128)(2,1)}), bf16[384,1024]{1,0:T(8,128)(2,1)}) %reduce-scatter.12.cloned.1.call-update) | async-done | bytes 786448
  492.8 65.0 %reduce-scatter.14.cloned.1.call-done = bf16[384,1024]{1,0:T(8,128)(2,1)} async-done(((bf16[3072,1024]{1,0:T(8,128)(2,1)}), bf16[384,1024]{1,0:T(8,128)(2,1)}) %reduce-scatter.14.cloned.1.call-update) | async-done | bytes 786448
  557.8 1.6 constant_dynamic-slice_fusion.3
  559.4 0.8 copy.17
  560.2 1.5 collective-permute-start.6
  561.7 0.8 copy.18
  562.5 0.5 collective-permute-start.7
  563.1 0.8 copy.19
  563.9 0.2 copy.16
  564.0 0.2 copy.22
  564.2 0.2 copy.23
  564.4 0.2 copy.21
  564.5 0.2 copy.20
  564.7 1.5 collective-permute-start.8
  566.2 2.4 collective-permute-start.10
  568.7 16.4 %collective-permute-done.6 = bf16[384,256]{0,1:T(8,128)(2,1)S(1)} collective-permute-done((bf16[384,256]{0,1:T(8,128)(2,1)}, bf16[384,256]{0,1:T(8,128)(2,1)S(1)}, u32[]{:S(2)}, u32[]{:S(2)}) %collective-permute-start.6) | collective-permute-done | bytes 196640 | tf_op jit(solution)/shard_map/ppermute | solution.py:31
  585.1 0.1 convert_add_fusion.1
  585.2 6.0 collective-permute-done.10
  591.3 4.1 collective-permute-done.11
  595.4 1.1 collective-permute-done.9
  596.7 1.4 copy.5
  (47 shorter events, 0.6 us)
Async XLA Ops:
  6.5 98.4 %all-gather.4.cloned.1.call-start = ((), (), s32[]{:S(2)}) async-start(), calls=%async_computation.3 | async-start | bytes 14155776 | tf_op jit(solution)/shard_map/all_gather | solution.py:46
  10.4 176.2 %all-gather.6.cloned.1.call-start = ((), (), s32[]{:S(2)}) async-start(), calls=%async_computation.4 | async-start | bytes 21233664 | tf_op jit(solution)/shard_map/all_gather | solution.py:50
  11.9 41.6 %collective-permute-start = (bf16[768,384]{1,0:T(8,128)(2,1)S(1)}, bf16[768,384]{1,0:T(8,128)(2,1)}, u32[]{:S(2)}, u32[]{:S(2)}) collective-permute-start(bf16[768,384]{1,0:T(8,128)(2,1)S(1)} %get-tuple-element.10), channel_id=1, source_target_pairs={{0,1},{1,2},{2,3},{3,0},{4,5},{5,6},{6,7},{7,4},{8,9},{9,10},{10,1... | collective-permute-start | bytes 1769480 | tf_op jit(solution)/shard_map/ppermute | solution.py:17
  13.5 41.2 %collective-permute-start.1 = (bf16[768,384]{1,0:T(8,128)(2,1)S(1)}, bf16[768,384]{1,0:T(8,128)(2,1)}, u32[]{:S(2)}, u32[]{:S(2)}) collective-permute-start(bf16[768,384]{1,0:T(8,128)(2,1)S(1)} %get-tuple-element.10), channel_id=1, source_target_pairs={{0,2},{1,3},{2,0},{3,1},{4,6},{5,7},{6,4},{7,5},{8,10},{9,11},{10,... | collective-permute-start | bytes 1769480 | tf_op jit(solution)/shard_map/ppermute | solution.py:17
  13.8 49.9 %collective-permute-start.2 = (bf16[768,384]{1,0:T(8,128)(2,1)S(1)}, bf16[768,384]{1,0:T(8,128)(2,1)S(1)}, u32[]{:S(2)}, u32[]{:S(2)}) collective-permute-start(bf16[768,384]{1,0:T(8,128)(2,1)S(1)} %get-tuple-element.10), channel_id=1, source_target_pairs={{0,3},{1,0},{2,1},{3,2},{4,7},{5,4},{6,5},{7,6},{8,11},{9,8},{10,9... | collective-permute-start | bytes 1769480 | tf_op jit(solution)/shard_map/ppermute | solution.py:17
  63.9 1.4 copy-start.2
  65.3 217.0 %all-gather.8.cloned.1.call-start = ((), (), s32[]{:S(2)}) async-start(), calls=%async_computation.5 | async-start | bytes 14155776 | tf_op jit(solution)/shard_map/all_gather | solution.py:53
  186.6 291.5 %reduce-scatter.10.cloned.1.call-start = ((), (), s32[]{:S(2)}) async-start(), calls=%async_computation.6 | async-start | bytes 7077888
  186.8 46.2 %copy-start = (f32[256,8,8,256]{3,1,2,0:T(8,128)S(1)}, f32[256,8,8,256]{3,1,2,0:T(8,128)}, u32[]{:S(2)}) copy-start(f32[256,8,8,256]{3,1,2,0:T(8,128)} %copy.24) | copy-start | bytes 50331652
  282.3 11.1 %copy-start.1 = (bf16[3072,2048]{1,0:T(8,128)(2,1)S(1)}, bf16[3072,2048]{1,0:T(8,128)(2,1)}, u32[]{:S(2)}) copy-start(bf16[3072,2048]{1,0:T(8,128)(2,1)} %all-gather.8.cloned.1.call-done) | copy-start | bytes 37748740
  365.9 126.9 %reduce-scatter.12.cloned.1.call-start = ((), (), s32[]{:S(2)}) async-start(), calls=%async_computation.7 | async-start | bytes 7077888
  365.9 14.8 %copy-start.4 = (bf16[4,1,256,2048]{3,2,1,0:T(8,128)(2,1)S(1)}, bf16[4,1,256,2048]{3,2,1,0:T(8,128)(2,1)}, u32[]{:S(2)}) copy-start(bf16[4,1,256,2048]{3,2,1,0:T(8,128)(2,1)} %get-tuple-element.15) | copy-start | bytes 12582916
  365.9 30.1 %slice-start = ((s8[12582912]{0:T(1024)(128)(4,1)}), s8[4194304]{0:T(1024)(128)(4,1)S(1)}, s32[]{:S(2)}) async-start(s8[12582912]{0:T(1024)(128)(4,1)} %bitcast.85), calls=%async_computation.9 | async-start | bytes 8388608
  365.9 30.1 %slice-start.1 = ((s8[12582912]{0:T(1024)(128)(4,1)}), s8[4194304]{0:T(1024)(128)(4,1)S(1)}, s32[]{:S(2)}) async-start(s8[12582912]{0:T(1024)(128)(4,1)} %bitcast.85), calls=%async_computation.10 | async-start | bytes 8388608
  380.7 15.3 %slice-start.2 = ((s8[12582912]{0:T(1024)(128)(4,1)}), s8[4194304]{0:T(1024)(128)(4,1)S(1)}, s32[]{:S(2)}) async-start(s8[12582912]{0:T(1024)(128)(4,1)} %bitcast.85), calls=%async_computation.11 | async-start | bytes 8388608
  421.5 136.3 %reduce-scatter.14.cloned.1.call-start = ((), (), s32[]{:S(2)}) async-start(), calls=%async_computation.8 | async-start | bytes 7077888
  421.5 14.9 %copy-start.3 = (bf16[4,1,256,2048]{3,2,1,0:T(8,128)(2,1)S(1)}, bf16[4,1,256,2048]{3,2,1,0:T(8,128)(2,1)}, u32[]{:S(2)}) copy-start(bf16[4,1,256,2048]{3,2,1,0:T(8,128)(2,1)} %get-tuple-element.14) | copy-start | bytes 12582916
  421.5 31.1 %slice-start.3 = ((s8[12582912]{0:T(1024)(128)(4,1)}), s8[4194304]{0:T(1024)(128)(4,1)S(1)}, s32[]{:S(2)}) async-start(s8[12582912]{0:T(1024)(128)(4,1)} %bitcast.87), calls=%async_computation.12 | async-start | bytes 8388608
  421.6 31.1 %slice-start.4 = ((s8[12582912]{0:T(1024)(128)(4,1)}), s8[4194304]{0:T(1024)(128)(4,1)S(1)}, s32[]{:S(2)}) async-start(s8[12582912]{0:T(1024)(128)(4,1)} %bitcast.87), calls=%async_computation.13 | async-start | bytes 8388608
  436.5 16.2 %slice-start.5 = ((s8[12582912]{0:T(1024)(128)(4,1)}), s8[4194304]{0:T(1024)(128)(4,1)S(1)}, s32[]{:S(2)}) async-start(s8[12582912]{0:T(1024)(128)(4,1)} %bitcast.87), calls=%async_computation.14 | async-start | bytes 8388608
  479.6 85.2 %collective-permute-start.3 = (bf16[384,256]{0,1:T(8,128)(2,1)S(1)}, bf16[384,256]{0,1:T(8,128)(2,1)S(1)}, u32[]{:S(2)}, u32[]{:S(2)}) collective-permute-start(bf16[384,256]{0,1:T(8,128)(2,1)S(1)} %copy.13), channel_id=1, source_target_pairs={{0,1},{1,2},{2,3},{3,0},{4,5},{5,6},{6,7},{7,4},{8,9},{9,10},{10,1... | collective-permute-start | bytes 589832 | tf_op jit(solution)/shard_map/ppermute | solution.py:31
  481.3 84.9 %collective-permute-start.4 = (bf16[384,256]{0,1:T(8,128)(2,1)S(1)}, bf16[384,256]{0,1:T(8,128)(2,1)S(1)}, u32[]{:S(2)}, u32[]{:S(2)}) collective-permute-start(bf16[384,256]{0,1:T(8,128)(2,1)S(1)} %copy.14), channel_id=1, source_target_pairs={{0,2},{1,3},{2,0},{3,1},{4,6},{5,7},{6,4},{7,5},{8,10},{9,11},{10,... | collective-permute-start | bytes 589832 | tf_op jit(solution)/shard_map/ppermute | solution.py:31
  482.0 86.6 %collective-permute-start.5 = (bf16[384,256]{0,1:T(8,128)(2,1)S(1)}, bf16[384,256]{0,1:T(8,128)(2,1)S(1)}, u32[]{:S(2)}, u32[]{:S(2)}) collective-permute-start(bf16[384,256]{0,1:T(8,128)(2,1)S(1)} %copy.15), channel_id=1, source_target_pairs={{0,3},{1,0},{2,1},{3,2},{4,7},{5,4},{6,5},{7,6},{8,11},{9,8},{10,9... | collective-permute-start | bytes 589832 | tf_op jit(solution)/shard_map/ppermute | solution.py:31
  560.2 24.9 %collective-permute-start.6 = (bf16[384,256]{0,1:T(8,128)(2,1)}, bf16[384,256]{0,1:T(8,128)(2,1)S(1)}, u32[]{:S(2)}, u32[]{:S(2)}) collective-permute-start(bf16[384,256]{0,1:T(8,128)(2,1)} %copy.17), channel_id=1, source_target_pairs={{0,1},{1,2},{2,3},{3,0},{4,5},{5,6},{6,7},{7,4},{8,9},{9,10},{10,1... | collective-permute-start | bytes 589832 | tf_op jit(solution)/shard_map/ppermute | solution.py:31
  562.5 22.6 %collective-permute-start.7 = (bf16[384,256]{0,1:T(8,128)(2,1)}, bf16[384,256]{0,1:T(8,128)(2,1)S(1)}, u32[]{:S(2)}, u32[]{:S(2)}) collective-permute-start(bf16[384,256]{0,1:T(8,128)(2,1)} %copy.18), channel_id=1, source_target_pairs={{0,2},{1,3},{2,0},{3,1},{4,6},{5,7},{6,4},{7,5},{8,10},{9,11},{10,... | collective-permute-start | bytes 589832 | tf_op jit(solution)/shard_map/ppermute | solution.py:31
  564.7 20.4 %collective-permute-start.8 = (bf16[384,256]{0,1:T(8,128)(2,1)}, bf16[384,256]{0,1:T(8,128)(2,1)S(1)}, u32[]{:S(2)}, u32[]{:S(2)}) collective-permute-start(bf16[384,256]{0,1:T(8,128)(2,1)} %copy.19), channel_id=1, source_target_pairs={{0,3},{1,0},{2,1},{3,2},{4,7},{5,4},{6,5},{7,6},{8,11},{9,8},{10,9... | collective-permute-start | bytes 589832 | tf_op jit(solution)/shard_map/ppermute | solution.py:31
  566.2 25.0 %collective-permute-start.10 = (bf16[384,256]{0,1:T(8,128)(2,1)S(1)}, bf16[384,256]{0,1:T(8,128)(2,1)S(1)}, u32[]{:S(2)}, u32[]{:S(2)}) collective-permute-start(bf16[384,256]{0,1:T(8,128)(2,1)S(1)} %copy.22), channel_id=1, source_target_pairs={{0,2},{1,3},{2,0},{3,1},{4,6},{5,7},{6,4},{7,5},{8,10},{9,11},{10,... | collective-permute-start | bytes 589832 | tf_op jit(solution)/shard_map/ppermute | solution.py:31
  568.6 26.7 %collective-permute-start.11 = (bf16[384,256]{0,1:T(8,128)(2,1)S(1)}, bf16[384,256]{0,1:T(8,128)(2,1)S(1)}, u32[]{:S(2)}, u32[]{:S(2)}) collective-permute-start(bf16[384,256]{0,1:T(8,128)(2,1)S(1)} %copy.23), channel_id=1, source_target_pairs={{0,3},{1,0},{2,1},{3,2},{4,7},{5,4},{6,5},{7,6},{8,11},{9,8},{10,9... | collective-permute-start | bytes 589832 | tf_op jit(solution)/shard_map/ppermute | solution.py:31
  585.1 11.4 %collective-permute-start.9 = (bf16[384,256]{0,1:T(8,128)(2,1)S(1)}, bf16[384,256]{0,1:T(8,128)(2,1)S(1)}, u32[]{:S(2)}, u32[]{:S(2)}) collective-permute-start(bf16[384,256]{0,1:T(8,128)(2,1)S(1)} %copy.21), channel_id=1, source_target_pairs={{0,1},{1,2},{2,3},{3,0},{4,5},{5,6},{6,7},{7,4},{8,9},{9,10},{10,1... | collective-permute-start | bytes 589832 | tf_op jit(solution)/shard_map/ppermute | solution.py:31
Sparse Core Ops, SparseCore 0:
  10.5 75.4 all-gather.3
  87.9 98.5 all-gather.5
  188.4 74.4 all-gather.7
  366.0 61.7 reduce-scatter.9
  431.0 61.7 reduce-scatter.11
  496.0 61.7 reduce-scatter.13
where the time goes:
time: 613 us; the launch traced here: 605 us
  matrix products  254 us (41%)
  waiting for transfers between devices  221 us (36%)
  local copies, waits for them, and re-layouts  90.4 us (15%)
  between operations  14 us (2%)
  starting transfers between devices  13.2 us (2%)
  other arithmetic  12.7 us (2%)
    dot_general x6, matrix products, local(): lax.dot_general(rows, weighted[h], (((1,), (1,)), ((), ())), preferred_el...  89.1 us
    unnamed x9, waiting for transfers between devices  74.3 us
    all_gather x1, waiting for transfers between devices, local(): whole = lax.all_gather(strip, 'gx', axis=0, tiled=False)  72.7 us
    dot_general x2, matrix products, local(): lax.dot_general(dense, gathered[h], (((0,), (0,)), ((), ())), preferred_e...  67.8 us
    unnamed x39, local copies, waits for them, and re-layouts  61.5 us
    dot_general x3, matrix products, local(): lax.dot_general(collocation, contracted.astype(BF16), (((1,), (1,)), ((),...  50.9 us
    ppermute x3, waiting for transfers between devices, spread(): got = lax.ppermute(block, axis, pairs)  46.2 us
    dot_general x1, matrix products, local(): lax.dot_general(whole, collocation.reshape(n_gx, cols, panel_rows), (((0,...  46.2 us
  transfers between devices with their start and end apart: 18, of which 9 were waited for; matrix products, arithmetic and copies ran while one was open for 44% of the time, Pallas kernels for 0%

commit v1 on v0

v1 whole, which is shorter than its diff:
```python
import functools
import math

import jax
import jax.numpy as jnp
from jax import lax
from jax.experimental import pallas as pl
from jax.experimental.pallas import tpu as pltpu
from jax.sharding import PartitionSpec as P

F32 = jnp.float32
BF16 = jnp.bfloat16
MESH = pl.DeviceIdType.MESH


def largest_tile(size, limit):
    tile = limit
    while size % tile:
        tile //= 2
    return tile


def plan(n_gx, n_gy, nbf, rows, piece):
    s = type("Plan", (), {})()
    s.n_gx, s.n_gy, s.nbf, s.rows, s.piece = n_gx, n_gy, nbf, rows, piece
    s.bits = int(math.log2(n_gx)) - 1
    assert 2 << s.bits == n_gx and s.bits >= 1
    s.chips = n_gx // 2
    s.halves = 2 if piece % 256 == 0 else 1
    s.cw = piece // s.halves
    s.plane = nbf // n_gy
    s.strip = s.plane // n_gx
    s.mb = nbf // n_gx
    s.ch = 128 * s.bits
    s.chunks = nbf // s.ch
    s.per_plane = s.plane // s.ch
    s.units = sorted(
        ((r, h) for r in range(n_gx) for h in range(s.halves)),
        key=lambda u: (bin(u[0] >> 1).count("1"), u[1] if u[0] > 1 else 0, u[0] & 1, u[0], u[1]),
    )
    s.k_all = n_gx * piece
    s.k_half = s.k_all // 2
    s.t_rows = max(rows, nbf // 2 + 2 * s.ch)
    s.pt = largest_tile(rows, 512)
    s.zr = largest_tile(rows, 64)
    return s


def last_bit(s, p, d):
    order = [(p + t) % s.bits for t in range(s.bits)]
    return [q for q in order if d >> q & 1][-1]


def kernel_body(s, coll, dens, zk, out, dfull, gath, coll_v, dt, w, gbuf, r0, r1, rz, zin, zf,
                keep, ks, uf, sem_z, sem_zs, sem_d, sem_ds, sem_g, sem_gs, sem_l, sem_gu, sem_zin,
                sem_rd, sem_rds, sem_rs, sem_rss, sem_rz, sem_rzs, ready):
    i, j = lax.axis_index("gx"), lax.axis_index("gy")
    bits, nbf, halves, cw, ch, mb = s.bits, s.nbf, s.halves, s.cw, s.ch, s.mb
    bit = [lax.rem(i // (1 << t), 2) for t in range(bits + 1)]

    def flip(mask):
        index = i
        for t in range(bits + 1):
            if mask >> t & 1:
                index = index + (1 - 2 * bit[t]) * (1 << t)
        return index

    def plane_at(shift):
        return lax.rem(j + shift + s.n_gy, s.n_gy)

    def rows_at(start, size, unit=8):
        return pl.ds(pl.multiple_of(start, unit), size)

    def remote(src, dst, send, recv, gx, gy):
        return pltpu.make_async_remote_copy(
            src_ref=src, dst_ref=dst, send_sem=send, recv_sem=recv,
            device_id=(gx, gy), device_id_type=MESH)

    def hop(p, r):
        if r & 1:
            return r - 1, 1
        q = last_bit(s, p, r >> 1)
        return r - (2 << q), 2 << q

    own_cols = j * s.piece

    def own_piece(h, rws):
        return coll.at[rws, rows_at(own_cols + h * cw, cw, 128)]

    part_rows = nbf // bits

    def g_copy(h, p, r):
        src_r, mask = hop(p, r)
        rws = pl.ds(p * part_rows, part_rows)
        src = own_piece(h, rws) if src_r == 0 else gath.at[src_r * halves + h, rws]
        return remote(src, gath.at[r * halves + h, rws],
                      sem_gs.at[h, p, r], sem_g.at[h, p, r], flip(mask), j)

    def d_copy(t, p, r):
        src_r, mask = hop(p, r)
        start = plane_at(-t) * s.plane + flip(src_r) * s.strip
        ref = dfull.at[rows_at(start, s.strip), pl.ds(p * part_rows, part_rows)]
        return remote(ref, ref, sem_ds.at[t, p, r], sem_d.at[t, p, r], flip(mask), j)

    def z_copy(t):
        src = dens.at[rows_at(i * s.strip, s.strip)]
        dst = dfull.at[rows_at(j * s.plane + i * s.strip, s.strip)]
        return remote(src, dst, sem_zs.at[t], sem_z.at[t], i, plane_at(t))

    def onward(make, d):
        for p in range(bits):
            make(p, 2 * d + 1).start()
        for p in range(bits):
            for r in range(2, s.n_gx, 2):
                if hop(p, r)[0] == 2 * d:
                    make(p, r).start()

    for t in range(1, s.n_gy):
        z_copy(t).start()
    load_coll = pltpu.make_async_copy(coll, coll_v, sem_l.at[0])
    load_coll.start()
    load_dens = pltpu.make_async_copy(dens, r0.at[pl.ds(0, s.plane)], sem_l.at[1])
    load_dens.start()
    for p in range(bits):
        g_copy(0, p, 2 << p).start()
    for h in range(halves):
        for p in range(bits):
            g_copy(h, p, 1).start()

    rt = largest_tile(s.plane, 256) if s.plane % 384 else 384

    def dense(mu0):
        def step(n, carry):
            a, t = lax.rem(n, s.plane // rt), n // (s.plane // rt)
            block = jnp.dot(r0[rows_at(a * rt, rt, 128), :], coll_v[:, rows_at(t * s.pt, s.pt, 128)],
                            preferred_element_type=F32)
            dt[rows_at(t * s.pt, s.pt, 128), rows_at(mu0 + a * rt, rt, 128)] = block.T.astype(BF16)
            return carry
        lax.fori_loop(0, (s.plane // rt) * (s.rows // s.pt), step, 0)

    def z_load(n):
        return pltpu.make_async_copy(zk.at[rows_at(n * s.zr, s.zr)], zin.at[lax.rem(n, 2)],
                                     sem_zin.at[lax.rem(n, 2)])

    def spread_kernel():
        steps = s.rows // s.zr
        lanes = s.piece // 128

        def step(n, carry):
            @pl.when(n + 1 < steps)
            def _():
                z_load(n + 1).start()
            z_load(n).wait()
            block = zin[lax.rem(n, 2)].astype(F32).reshape(s.zr * s.n_gx, s.piece)
            for c in range(lanes):
                zf[c] = block[:, c * 128:(c + 1) * 128]
            for u, (r, h) in enumerate(s.units):
                k = flip(r)
                for c in range(cw // 128):
                    lane = zf[h * (cw // 128) + c, pl.ds(k, s.zr, stride=s.n_gx), :]
                    w[rows_at(n * s.zr, s.zr, 16), pl.ds(u * cw + c * 128, 128)] = lane.astype(BF16)
            return carry
        lax.fori_loop(0, steps, step, 0)

    z_load(0).start()
    load_coll.wait()
    load_dens.wait()
    dense(j * s.plane)

    chip_order = sorted(range(1, s.chips), key=lambda d: (bin(d).count("1"), d))

    def strip_on(t):
        z_copy(t).wait_recv()
        onward(functools.partial(d_copy, t), 0)

    def strips_on(t):
        for d in chip_order:
            for p in range(bits):
                d_copy(t, p, 2 * d).wait_recv()
            onward(functools.partial(d_copy, t), d)

    def dense_of(t):
        for d in range(s.chips):
            for p in range(bits):
                d_copy(t, p, 2 * d + 1).wait_recv()
        mu0 = plane_at(-t) * s.plane
        load = pltpu.make_async_copy(dfull.at[rows_at(mu0, s.plane, 128)], r0.at[pl.ds(0, s.plane)],
                                     sem_l.at[1])
        load.start()
        load.wait()
        dense(mu0)

    for t in range(1, s.n_gy):
        strip_on(t)
        if t == 1:
            spread_kernel()
        if t >= 2:
            strips_on(t - 1)
        if t >= 3:
            dense_of(t - 2)
    strips_on(s.n_gy - 1)
    for h in range(halves):
        for p in range(bits):
            if h > 0:
                g_copy(h, p, 2 << p).start()
        for p in range(bits):
            for q in range(bits):
                if q != p:
                    g_copy(h, p, 2 << q).start()
    for t in range(max(1, s.n_gy - 2), s.n_gy):
        dense_of(t)

    def fetch(u):
        r, h = s.units[u]
        slot = gbuf.at[u % 2, pl.ds(0, nbf), pl.ds(0, cw)]
        if r == 0:
            src = own_piece(h, pl.ds(0, nbf))
        else:
            src = gath.at[r * halves + h]
        return pltpu.make_async_copy(src, slot, sem_l.at[2 + u % 2])

    def arrive(u):
        r, h = s.units[u]
        if r:
            for p in range(bits):
                g_copy(h, p, r).wait_recv()
        if r and not r & 1:
            onward(functools.partial(g_copy, h), r >> 1)
        fetch(u).start()

    arrive(0)
    n_units, tiles = len(s.units), s.rows // s.pt

    def m_step(n, carry):
        u, t = n // tiles, lax.rem(n, tiles)
        slot = lax.rem(u, 2)

        @pl.when(t == 0)
        def _():
            pltpu.make_async_copy(gath.at[0], gbuf.at[slot, pl.ds(0, nbf), pl.ds(0, cw)],
                                  sem_l.at[2 + slot]).wait()

        for uu in range(1, n_units):
            @pl.when(jnp.logical_and(t == tiles // 2, u + 1 == uu))
            def _():
                arrive(uu)

        products = jnp.dot(dt[rows_at(t * s.pt, s.pt, 128), :], gbuf[slot, :nbf, :cw],
                           preferred_element_type=F32)
        place = (rows_at(t * s.pt, s.pt, 128), rows_at(u * cw, cw, 128))
        w[place] = (w[place].astype(F32) * products).astype(BF16)
        return carry
    lax.fori_loop(0, n_units * tiles, m_step, 0)

    masks = [1] + [2 << q for q in range(bits)]
    for t, mask in enumerate(masks):
        pl.semaphore_signal(ready.at[t], inc=1, device_id=(flip(mask), j), device_id_type=MESH)

    def chunk_plane(n):
        shift = n // s.per_plane + 1
        return lax.rem(j + shift, s.n_gy)

    def gu_copies(n, part):
        nu0 = chunk_plane(n) * s.plane + lax.rem(n, s.per_plane) * ch
        rws = rows_at(nu0, ch, 128)
        half = n_units // 2
        for u in range(part * half, (part + 1) * half):
            r, h = s.units[u]
            if r == 0:
                src = own_piece(h, rws)
            else:
                src = gath.at[r * halves + h, rws]
            dst = dt.at[pl.ds(nbf // 2 + part * ch, ch), pl.ds((u - part * half) * cw, cw)]
            yield pltpu.make_async_copy(src, dst, sem_gu.at[part, u - part * half])

    for part in range(2):
        for copy in gu_copies(0, part):
            copy.start()
    for t in range(bits + 1):
        pl.semaphore_wait(ready.at[t], 1)

    half_rows = nbf // 2
    send_d = gbuf.at[0, pl.ds(0, half_rows), pl.ds(0, ch)]
    u_v = gbuf.at[1, pl.ds(0, s.rows), pl.ds(0, ch)]
    send_at, at = [], half_rows
    for t in range(bits):
        size = (s.chips >> (t + 1)) * mb
        send_at.append((at, size))
        at += size
    sz = gbuf.at[0, pl.ds(at, mb), pl.ds(0, ch)]
    assert at + mb <= nbf
    recvs = [r0] + [r1[t] for t in range(bits - 1)]

    def cols(n):
        return rows_at(n * ch, ch, 128)

    def swap_copy(n):
        return remote(send_d, dt.at[pl.ds(0, half_rows), cols(n)], sem_rds.at[0], sem_rd.at[n],
                      flip(1), j)

    def halve_copy(n, t, p):
        q = (p + t) % bits
        at, size = send_at[t]
        return remote(gbuf.at[0, pl.ds(at, size), pl.ds(p * 128, 128)],
                      recvs[t].at[pl.ds(0, size), rows_at(n * ch + p * 128, 128, 128)],
                      sem_rss.at[t, p], sem_rs.at[n, t, p], flip(2 << q), j)

    def blocks(t, p):
        q = (p + t) % bits
        free = [f for f in range(bits) if f not in [(p + e) % bits for e in range(t)]]
        rest = [f for f in free if f != q]
        pairs = []
        for combo in range(1 << len(rest)):
            base = 0
            for e, f in enumerate(rest):
                base = base + (combo >> e & 1) * (1 << free.index(f))
            weight = 1 << free.index(q)
            mine = bit[q + 1]
            pairs.append((base + mine * weight, base + (1 - mine) * weight))
        return pairs

    def halve(n, t):
        held = keep if t == 0 else ks[t - 1]
        at, _ = send_at[t]

        for p in range(bits):
            lane = pl.ds(p * 128, 128)

            @pl.when(n >= 1)
            def _():
                halve_copy(n - 1, t, p).wait_send()
            for e, (kept, sent) in enumerate(blocks(t, p)):
                gbuf[0, pl.ds(at + e * mb, mb), lane] = held[rows_at(sent * mb, mb, 128), lane].astype(BF16)
            halve_copy(n, t, p).start()
            for e, (kept, sent) in enumerate(blocks(t, p)):
                ks[t][pl.ds(e * mb, mb), lane] = held[rows_at(kept * mb, mb, 128), lane]

    def take(n, t):
        _, size = send_at[t]
        for p in range(bits):
            halve_copy(n, t, p).wait_recv()
            lane = pl.ds(p * 128, 128)
            ks[t][pl.ds(0, size), lane] += recvs[t][
                pl.ds(0, size), rows_at(n * ch + p * 128, 128, 128)].astype(F32)

    def plane_copy(n):
        shift = n // s.per_plane + 1
        c = lax.rem(n, s.per_plane)
        dst = rz.at[rows_at((shift - 1) * mb, mb, 8), rows_at(c * ch, ch, 128)]
        return remote(sz, dst, sem_rzs.at[0], sem_rz.at[n], i, chunk_plane(n))

    away = (s.n_gy - 1) * s.per_plane

    def finish(n):
        total = ks[bits - 1]

        @pl.when(n < away)
        def _():
            @pl.when(n >= 1)
            def _():
                plane_copy(n - 1).wait_send()
            sz[...] = total[pl.ds(0, mb), :].astype(BF16)
            plane_copy(n).start()

        @pl.when(n >= away)
        def _():
            c = n - away
            for t in range(s.n_gy - 1):
                plane_copy(t * s.per_plane + c).wait_recv()
                total[pl.ds(0, mb), :] += rz[pl.ds(t * mb, mb), cols(c)].astype(F32)
            copy = pltpu.make_async_copy(total.at[pl.ds(0, mb)], out.at[:, cols(c)], sem_l.at[0])
            copy.start()
            copy.wait()

    core = bit[0]

    def b_step(n, carry):
        @pl.when(n < s.chunks)
        def _():
            for part in range(2):
                for copy in gu_copies(n, part):
                    copy.wait()

                def u_step(t, carry):
                    rws = rows_at(t * s.pt, s.pt, 128)
                    piece = lax.dot_general(
                        w[rws, pl.ds(part * s.k_half, s.k_half)],
                        dt[pl.ds(nbf // 2 + part * ch, ch), pl.ds(0, s.k_half)],
                        (((1,), (1,)), ((), ())), preferred_element_type=F32)
                    if part == 0:
                        uf[rws, :] = piece
                    else:
                        gbuf[1, rws, pl.ds(0, ch)] = (uf[rws, :] + piece).astype(BF16)
                    return carry
                lax.fori_loop(0, tiles, u_step, 0)

                @pl.when(n + 1 < s.chunks)
                def _():
                    for copy in gu_copies(n + 1, part):
                        copy.start()

        for t in reversed(range(bits)):
            m = n - 2 - t

            @pl.when(jnp.logical_and(m >= 0, m < s.chunks))
            def _():
                take(m, t)
                if t == bits - 1:
                    finish(m)
                else:
                    halve(m, t + 1)

        @pl.when(jnp.logical_and(n >= 1, n <= s.chunks))
        def _():
            swap_copy(n - 1).wait()
            keep[...] += dt[pl.ds(0, half_rows), cols(n - 1)].astype(F32)
            halve(n - 1, 0)

        @pl.when(n < s.chunks)
        def _():
            def t_block(q, side):
                return jnp.dot(coll_v[rows_at((2 * q + side) * mb, mb, 128), :],
                               gbuf[1, pl.ds(0, s.rows), pl.ds(0, ch)], preferred_element_type=F32)

            def sent(q, carry):
                gbuf[0, rows_at(q * mb, mb, 128), pl.ds(0, ch)] = t_block(q, 1 - core).astype(BF16)
                return carry
            lax.fori_loop(0, s.chips, sent, 0)
            swap_copy(n).start()

            def kept(q, carry):
                keep[rows_at(q * mb, mb, 128), :] = t_block(q, core)
                return carry
            lax.fori_loop(0, s.chips, kept, 0)
        return carry
    lax.fori_loop(0, s.chunks + bits + 1, b_step, 0)

    plane_copy(away - 1).wait_send()
    for t in range(bits):
        for p in range(bits):
            halve_copy(s.chunks - 1, t, p).wait_send()
    for t in range(1, s.n_gy):
        z_copy(t).wait_send()
    for r in range(1, s.n_gx):
        for p in range(bits):
            for t in range(1, s.n_gy):
                d_copy(t, p, r).wait_send()
            for h in range(halves):
                g_copy(h, p, r).wait_send()


def build(n_gx, n_gy):
    def local(collocation, density, kernel):
        nbf, rows = collocation.shape
        s = plan(n_gx, n_gy, nbf, rows, kernel.shape[3])
        zk = kernel.reshape(rows, n_gx, kernel.shape[3])
        any_spec = pl.BlockSpec(memory_space=pl.ANY)
        dma = pltpu.SemaphoreType.DMA
        wide = max(s.cw, s.ch)
        r1 = [pltpu.VMEM(((s.chips >> (t + 1)) * s.mb, nbf), BF16) for t in range(1, s.bits)]
        ks = [pltpu.VMEM(((s.chips >> (t + 1)) * s.mb, s.ch), F32) for t in range(s.bits)]
        out = pl.pallas_call(
            functools.partial(kernel_body, s),
            out_shape=(
                jax.ShapeDtypeStruct((s.mb, s.plane), F32),
                jax.ShapeDtypeStruct((nbf, nbf), BF16),
                jax.ShapeDtypeStruct((n_gx * s.halves, nbf, s.cw), BF16),
            ),
            in_specs=[any_spec] * 3,
            out_specs=(any_spec,) * 3,
            scratch_shapes=[
                pltpu.VMEM((nbf, rows), BF16),
                pltpu.VMEM((s.t_rows, nbf), BF16),
                pltpu.VMEM((rows, s.k_all), BF16),
                pltpu.VMEM((2, nbf, wide), BF16),
                pltpu.VMEM((max(s.plane, (s.chips // 2) * s.mb), nbf), BF16),
                r1,
                pltpu.VMEM(((n_gy - 1) * s.mb, s.plane), BF16),
                pltpu.VMEM((2, s.zr, n_gx, s.piece), BF16),
                pltpu.VMEM((s.piece // 128, s.zr * n_gx, 128), F32),
                pltpu.VMEM((nbf // 2, s.ch), F32),
                ks,
                pltpu.VMEM((rows, s.ch), F32),
                dma((n_gy,)),
                dma((n_gy,)),
                dma((n_gy, s.bits, n_gx)),
                dma((n_gy, s.bits, n_gx)),
                dma((s.halves, s.bits, n_gx)),
                dma((s.halves, s.bits, n_gx)),
                dma((4,)),
                dma((2, len(s.units) // 2)),
                dma((2,)),
                dma((s.chunks,)),
                dma((1,)),
                dma((s.chunks, s.bits, s.bits)),
                dma((s.bits, s.bits)),
                dma((s.chunks,)),
                dma((1,)),
                pltpu.SemaphoreType.REGULAR((s.bits + 1,)),
            ],
            compiler_params=pltpu.CompilerParams(
                has_side_effects=True, vmem_limit_bytes=67043328),
            name="exchange",
        )(collocation, density, zk)
        return out[0]

    return local


def solution(mesh):
    return jax.shard_map(
        build(mesh.shape["gx"], mesh.shape["gy"]),
        mesh=mesh,
        in_specs=(P(None, "gx"), P("gy", None), P("gx", None, "gy", None)),
        out_specs=P("gx", "gy"),
        check_vma=False,
    )
```

time: 613 us -> 382 us (0.62); the launches traced: 605 us -> 381 us
  Pallas kernels: 0 us -> 379 us
  matrix products: 254 us -> 0 us
  waiting for transfers between devices: 221 us -> 0 us
  local copies, waits for them, and re-layouts: 90.4 us -> 2.36 us
  between operations: 14 us -> 0.01 us
  starting transfers between devices: 13.2 us -> 0 us
  other arithmetic: 12.7 us -> 0 us
    pallas_call x0 -> x1, Pallas kernels: none -> 379 us  [local(): pl.pallas_call(functools.partial(kernel_body, s), out_shape=(jax.ShapeDty...]
    dot_general x12 -> x0, matrix products: 254 us -> none  [the longest x6 89.1 us: local(): lax.dot_general(rows, weighted[h], (((1,), (1,)), ((), ())), preferred_el...]
    unnamed x9 -> x0, waiting for transfers between devices: 74.3 us -> none
    ppermute x12 -> x0, waiting for transfers between devices: 73.9 us -> none  [the longest x3 46.2 us: spread(): got = lax.ppermute(block, axis, pairs)]
    all_gather x3 -> x0, waiting for transfers between devices: 72.7 us -> none  [the longest x1 72.7 us: local(): whole = lax.all_gather(strip, 'gx', axis=0, tiled=False)]
    unnamed x39 -> x1, local copies, waits for them, and re-layouts: 61.5 us -> 2.36 us
    slice x2 -> x0, local copies, waits for them, and re-layouts: 17 us -> none  [local(): gathered[h].reshape(n_gy, parts, sub, -1)[:, c].reshape(n_gy * sub, -1)]
    ppermute x12 -> x0, starting transfers between devices: 12.8 us -> none  [the longest x9 9.53 us: exchange_sum(): total = total + lax.ppermute(sent, axis, pairs).astype(F32)]
  transfers between devices with their start and end apart: 18 -> 0, of which waited for: 9 -> 0; matrix products, arithmetic and copies ran while one was open for 44% -> 0% of each run, Pallas kernels for 0% -> 0%
where the time goes in v1:
time: 382 us; the launch traced here: 381 us
  Pallas kernels  379 us (99%)
    pallas_call x1, Pallas kernels, local(): pl.pallas_call(functools.partial(kernel_body, s), out_shape=(jax.ShapeDty...  379 us

profile of v1, /device:TPU:18, one launch (start us, length us, event | category | flops | bytes accessed | tf_op | source)
XLA Modules:
  0.0 381.1 jit_solution(8082016683409621121)
XLA Ops:
  0.0 378.8 %exchange.1 = (f32[384,768]{1,0:T(8,128)}, bf16[3072,3072]{1,0:T(8,128)(2,1)}, bf16[16,3072,256]{2,1,0:T(8,128)(2,1)}) custom-call(bf16[3072,2048]{1,0:T(8,128)(2,1)} %coll.1, bf16[768,3072]{1,0:T(8,128)(2,1)} %dens.1, bf16[2048,8,512]{2,1,0:T(8,128)(2,1)} %bitcast.1), custom_call_target="tpu_custom_call" | custom-call | tf_op jit(solution)/shard_map/exchange/pallas_call | solution.py:462
  378.8 2.4 copy.5

commit v2 on v1

--- a/solution.py
+++ b/solution.py
@@ -41,8 +41,12 @@
     s.k_all = n_gx * piece
     s.k_half = s.k_all // 2
     s.t_rows = max(rows, nbf // 2 + 2 * s.ch)
-    s.pt = largest_tile(rows, 512)
-    s.zr = largest_tile(rows, 64)
+    s.pt = largest_tile(rows, 1024)
+    s.sorted_rows = s.mb % 128 == 0
+    s.tt = largest_tile(nbf // 2, 768) if s.sorted_rows else s.mb
+    s.near = [sorted((p for p in range(n_gy) if p != m), key=lambda p: (abs(p - m), p))
+              for m in range(n_gy)]
+    s.zr = largest_tile(rows, 128)
     return s
 
 
@@ -51,9 +55,9 @@
     return [q for q in order if d >> q & 1][-1]
 
 
-def kernel_body(s, coll, dens, zk, out, dfull, gath, coll_v, dt, w, gbuf, r0, r1, rz, zin, zf,
-                keep, ks, uf, sem_z, sem_zs, sem_d, sem_ds, sem_g, sem_gs, sem_l, sem_gu, sem_zin,
-                sem_rd, sem_rds, sem_rs, sem_rss, sem_rz, sem_rzs, ready):
+def kernel_body(s, coll, dens, zk, out, dfull, gath, upart, coll_v, dt, w, gbuf, r0, r1, rz, zin, zf,
+                keep, ks, uf, sem_up, sem_z, sem_zs, sem_d, sem_ds, sem_g, sem_gs, sem_l, sem_gu, sem_zin,
+                sem_rd, sem_rds, sem_rs, sem_rss, sem_rz, sem_rzs, sem_lc, sem_ld, ready):
     i, j = lax.axis_index("gx"), lax.axis_index("gy")
     bits, nbf, halves, cw, ch, mb = s.bits, s.nbf, s.halves, s.cw, s.ch, s.mb
     bit = [lax.rem(i // (1 << t), 2) for t in range(bits + 1)]
@@ -65,8 +69,11 @@
                 index = index + (1 - 2 * bit[t]) * (1 << t)
         return index
 
-    def plane_at(shift):
-        return lax.rem(j + shift + s.n_gy, s.n_gy)
+    def near_plane(t):
+        plane = 0
+        for m in range(s.n_gy):
+            plane = plane + jnp.where(j == m, s.near[m][t - 1], 0)
+        return plane
 
     def rows_at(start, size, unit=8):
         return pl.ds(pl.multiple_of(start, unit), size)
@@ -98,29 +105,73 @@
 
     def d_copy(t, p, r):
         src_r, mask = hop(p, r)
-        start = plane_at(-t) * s.plane + flip(src_r) * s.strip
+        start = near_plane(t) * s.plane + flip(src_r) * s.strip
         ref = dfull.at[rows_at(start, s.strip), pl.ds(p * part_rows, part_rows)]
         return remote(ref, ref, sem_ds.at[t, p, r], sem_d.at[t, p, r], flip(mask), j)
 
-    def z_copy(t):
-        src = dens.at[rows_at(i * s.strip, s.strip)]
-        dst = dfull.at[rows_at(j * s.plane + i * s.strip, s.strip)]
-        return remote(src, dst, sem_zs.at[t], sem_z.at[t], i, plane_at(t))
-
-    def onward(make, d):
-        for p in range(bits):
-            make(p, 2 * d + 1).start()
-        for p in range(bits):
-            for r in range(2, s.n_gx, 2):
-                if hop(p, r)[0] == 2 * d:
-                    make(p, r).start()
-
-    for t in range(1, s.n_gy):
-        z_copy(t).start()
-    load_coll = pltpu.make_async_copy(coll, coll_v, sem_l.at[0])
-    load_coll.start()
-    load_dens = pltpu.make_async_copy(dens, r0.at[pl.ds(0, s.plane)], sem_l.at[1])
-    load_dens.start()
+    inner = jnp.logical_and(j > 0, j < s.n_gy - 1)
+
+    def part_cols(p):
+        return pl.ds(p * part_rows, part_rows)
+
+    def strip_rows(plane, p):
+        return dfull.at[rows_at(plane * s.plane + i * s.strip, s.strip), part_cols(p)]
+
+    def z_copy(t, step, p):
+        plane = near_plane(t) if t else j
+        src = strip_rows(plane, p) if t else dens.at[rows_at(i * s.strip, s.strip), part_cols(p)]
+        return remote(src, strip_rows(plane, p), sem_zs.at[2 * t + (step > 0), p],
+                      sem_z.at[plane, p], i, j + step)
+
+    def z_sends(act):
+        for step in (1, -1):
+            @pl.when(j + step < s.n_gy if step > 0 else j > 0)
+            def _():
+                for p in range(bits):
+                    act(z_copy(0, step, p))
+
+    def z_relays(t, p, act):
+        for step in (1, -1):
+            plane = near_plane(t)
+
+            @pl.when(jnp.logical_and(inner, plane < j if step > 0 else plane > j))
+            def _():
+                act(z_copy(t, step, p))
+
+    def z_arrived(t, p):
+        plane = near_plane(t)
+        ref = strip_rows(plane, p)
+        remote(ref, ref, sem_zs.at[0, p], sem_z.at[plane, p], i, plane).wait_recv()
+
+    def onward(make, d, p):
+        for r in range(2, s.n_gx, 2):
+            if hop(p, r)[0] == 2 * d:
+                make(p, r).start()
+        make(p, 2 * d + 1).start()
+
+    z_sends(lambda copy: copy.start())
+    core = bit[0]
+
+    def sorted_blocks():
+        if not s.sorted_rows:
+            return [(0, 0, nbf)]
+        places = []
+        for side in range(2):
+            for q in range(s.chips):
+                places.append((side * (nbf // 2) + q * mb, (2 * q + (1 - core if side == 0 else core)) * mb, mb))
+        return places
+
+    places = sorted_blocks()
+    load_coll = [pltpu.make_async_copy(coll.at[rows_at(src, size, 128)], coll_v.at[pl.ds(at, size)],
+                                       sem_lc.at[e]) for e, (at, src, size) in enumerate(places)]
+
+    def load_density(ref, row):
+        return [pltpu.make_async_copy(ref.at[rows_at(row, s.plane, 128), rows_at(src, size, 128)],
+                                      r0.at[pl.ds(0, s.plane), pl.ds(at, size)], sem_ld.at[e])
+                for e, (at, src, size) in enumerate(places)]
+
+    for copy in load_coll + load_density(dens, 0):
+        copy.start()
     for p in range(bits):
         g_copy(0, p, 2 << p).start()
     for h in range(halves):
@@ -142,8 +193,9 @@
         return pltpu.make_async_copy(zk.at[rows_at(n * s.zr, s.zr)], zin.at[lax.rem(n, 2)],
                                      sem_zin.at[lax.rem(n, 2)])
 
-    def spread_kernel():
-        steps = s.rows // s.zr
+    steps = s.rows // s.zr
+
+    def spread_kernel(first, last):
         lanes = s.piece // 128
 
         def step(n, carry):
@@ -160,44 +212,51 @@
                     lane = zf[h * (cw // 128) + c, pl.ds(k, s.zr, stride=s.n_gx), :]
                     w[rows_at(n * s.zr, s.zr, 16), pl.ds(u * cw + c * 128, 128)] = lane.astype(BF16)
             return carry
-        lax.fori_loop(0, steps, step, 0)
+        lax.fori_loop(first, last, step, 0)
 
     z_load(0).start()
-    load_coll.wait()
-    load_dens.wait()
+    for copy in load_coll + load_density(dens, 0):
+        copy.wait()
     dense(j * s.plane)
 
     chip_order = sorted(range(1, s.chips), key=lambda d: (bin(d).count("1"), d))
 
     def strip_on(t):
-        z_copy(t).wait_recv()
-        onward(functools.partial(d_copy, t), 0)
+        for p in range(bits):
+            z_arrived(t, p)
+            z_relays(t, p, lambda copy: copy.start())
+            onward(functools.partial(d_copy, t), 0, p)
 
     def strips_on(t):
         for d in chip_order:
-            for p in range(bits):
+            for p in sorted(range(bits), key=lambda p: hop(p, 2 * d)[0]):
                 d_copy(t, p, 2 * d).wait_recv()
-            onward(functools.partial(d_copy, t), d)
+                onward(functools.partial(d_copy, t), d, p)
 
     def dense_of(t):
         for d in range(s.chips):
             for p in range(bits):
                 d_copy(t, p, 2 * d + 1).wait_recv()
-        mu0 = plane_at(-t) * s.plane
-        load = pltpu.make_async_copy(dfull.at[rows_at(mu0, s.plane, 128)], r0.at[pl.ds(0, s.plane)],
-                                     sem_l.at[1])
-        load.start()
-        load.wait()
+        mu0 = near_plane(t) * s.plane
+        for copy in load_density(dfull, mu0):
+            copy.start()
+        for copy in load_density(dfull, mu0):
+            copy.wait()
         dense(mu0)
 
     for t in range(1, s.n_gy):
-        strip_on(t)
-        if t == 1:
-            spread_kernel()
+        if t in (2, 3):
+            pl.when(inner)(lambda: strip_on(t))
+            spread_kernel((t - 2) * steps // 2, (t - 1) * steps // 2)
+            pl.when(jnp.logical_not(inner))(lambda: strip_on(t))
+        else:
+            strip_on(t)
         if t >= 2:
             strips_on(t - 1)
         if t >= 3:
             dense_of(t - 2)
+    if s.n_gy < 4:
+        spread_kernel(max(s.n_gy - 2, 0) * steps // 2, steps)
     strips_on(s.n_gy - 1)
     for h in range(halves):
         for p in range(bits):
@@ -219,63 +278,127 @@
             src = gath.at[r * halves + h]
         return pltpu.make_async_copy(src, slot, sem_l.at[2 + u % 2])
 
+    n_units, tiles, half = len(s.units), s.rows // s.pt, len(s.units) // 2
+    ahead = 4
+
+    def by_link(u):
+        return 0 < u < n_units and s.units[u][0] > 1 and not s.units[u][0] & 1
+
+    def pass_on(u):
+        r, h = s.units[u]
+        for p in range(bits):
+            g_copy(h, p, r).wait_recv()
+            onward(functools.partial(g_copy, h), r >> 1, p)
+
     def arrive(u):
         r, h = s.units[u]
-        if r:
+        if r & 1:
             for p in range(bits):
                 g_copy(h, p, r).wait_recv()
-        if r and not r & 1:
-            onward(functools.partial(g_copy, h), r >> 1)
         fetch(u).start()
 
+    def m_loop(first, last):
+        def m_step(n, carry):
+            u, t = n // tiles, lax.rem(n, tiles)
+            slot = lax.rem(u, 2)
+
+            @pl.when(t == 0)
+            def _():
+                pltpu.make_async_copy(gath.at[0], gbuf.at[slot, pl.ds(0, nbf), pl.ds(0, cw)],
+                                      sem_l.at[2 + slot]).wait()
+
+            for uu in range(first, last):
+                onto = uu + ahead if by_link(uu + ahead) and (uu + ahead < last or last == n_units) else 0
+                if onto or uu + 1 < last:
+                    @pl.when(jnp.logical_and(t == tiles // 2, u == uu))
+                    def _():
+                        if onto:
+                            pass_on(onto)
+                        if uu + 1 < last:
+                            arrive(uu + 1)
+
+            products = jnp.dot(dt[rows_at(t * s.pt, s.pt, 128), :], gbuf[slot, :nbf, :cw],
+                               preferred_element_type=F32)
+            place = (rows_at(t * s.pt, s.pt, 128), rows_at(u * cw, cw, 128))
+            w[place] = (w[place].astype(F32) * products).astype(BF16)
+            return carry
+        lax.fori_loop(first * tiles, last * tiles, m_step, 0)
+
+    def chunk_plane(n):
+        shift = n // s.per_plane + 1
+        return lax.rem(j + shift, s.n_gy)
+
+    def gu_copies(n, part, slot, buffer, row):
+        nu0 = chunk_plane(n) * s.plane + lax.rem(n, s.per_plane) * ch
+        rws = rows_at(nu0, ch, 128)
+        for e in range(half):
+            r, h = s.units[part * half + e]
+            src = own_piece(h, rws) if r == 0 else gath.at[r * halves + h, rws]
+            dst = buffer.at[rows_at(row + slot * ch, ch, 128), pl.ds(e * cw, cw)]
+            yield pltpu.make_async_copy(src, dst, sem_gu.at[slot, e])
+
+    def u_product(n, t, part, buffer, row):
+        return lax.dot_general(
+            w[rows_at(t * s.pt, s.pt, 128), pl.ds(part * s.k_half, s.k_half)],
+            buffer[rows_at(row + lax.rem(n, 2) * ch, ch, 128), pl.ds(0, s.k_half)],
+            (((1,), (1,)), ((), ())), preferred_element_type=F32)
+
+    def half_u():
+        def store(n, t):
+            rws = rows_at(t * s.pt, s.pt, 128)
+            return pltpu.make_async_copy(uf.at[rws], upart.at[n, rws], sem_up.at[t])
+
+        for copy in gu_copies(0, 0, 0, r0, 0):
+            copy.start()
+
+        def step(n, carry):
+            slot = lax.rem(n, 2)
+            for copy in gu_copies(n, 0, slot, r0, 0):
+                copy.wait()
+
+            @pl.when(n + 1 < s.chunks)
+            def _():
+                for copy in gu_copies(n + 1, 0, 1 - slot, r0, 0):
+                    copy.start()
+
+            @pl.when(n == s.chunks // 2 - 1)
+            def _():
+                for u in range(half, half + ahead):
+                    if by_link(u):
+                        pass_on(u)
+
+            def u_step(t, carry):
+                @pl.when(n >= 1)
+                def _():
+                    store(n - 1, t).wait()
+                uf[rows_at(t * s.pt, s.pt, 128), :] = u_product(n, t, 0, r0, 0)
+                store(n, t).start()
+                return carry
+            lax.fori_loop(0, tiles, u_step, 0)
+            return carry
+        lax.fori_loop(0, s.chunks, step, 0)
+        for t in range(tiles):
+            store(s.chunks - 1, t).wait()
+
+    for u in range(min(ahead, half)):
+        if by_link(u):
+            pass_on(u)
     arrive(0)
-    n_units, tiles = len(s.units), s.rows // s.pt
-
-    def m_step(n, carry):
-        u, t = n // tiles, lax.rem(n, tiles)
-        slot = lax.rem(u, 2)
-
-        @pl.when(t == 0)
-        def _():
-            pltpu.make_async_copy(gath.at[0], gbuf.at[slot, pl.ds(0, nbf), pl.ds(0, cw)],
-                                  sem_l.at[2 + slot]).wait()
-
-        for uu in range(1, n_units):
-            @pl.when(jnp.logical_and(t == tiles // 2, u + 1 == uu))
-            def _():
-                arrive(uu)
-
-        products = jnp.dot(dt[rows_at(t * s.pt, s.pt, 128), :], gbuf[slot, :nbf, :cw],
-                           preferred_element_type=F32)
-        place = (rows_at(t * s.pt, s.pt, 128), rows_at(u * cw, cw, 128))
-        w[place] = (w[place].astype(F32) * products).astype(BF16)
-        return carry
-    lax.fori_loop(0, n_units * tiles, m_step, 0)
+    m_loop(0, half)
+    half_u()
+    arrive(half)
+    m_loop(half, n_units)
 
     masks = [1] + [2 << q for q in range(bits)]
     for t, mask in enumerate(masks):
         pl.semaphore_signal(ready.at[t], inc=1, device_id=(flip(mask), j), device_id_type=MESH)
 
-    def chunk_plane(n):
-        shift = n // s.per_plane + 1
-        return lax.rem(j + shift, s.n_gy)
-
-    def gu_copies(n, part):
-        nu0 = chunk_plane(n) * s.plane + lax.rem(n, s.per_plane) * ch
-        rws = rows_at(nu0, ch, 128)
-        half = n_units // 2
-        for u in range(part * half, (part + 1) * half):
-            r, h = s.units[u]
-            if r == 0:
-                src = own_piece(h, rws)
-            else:
-                src = gath.at[r * halves + h, rws]
-            dst = dt.at[pl.ds(nbf // 2 + part * ch, ch), pl.ds((u - part * half) * cw, cw)]
-            yield pltpu.make_async_copy(src, dst, sem_gu.at[part, u - part * half])
-
-    for part in range(2):
-        for copy in gu_copies(0, part):
-            copy.start()
+    def load_u(n):
+        return pltpu.make_async_copy(upart.at[n], uf, sem_up.at[0])
+
+    for copy in gu_copies(0, 1, 0, dt, nbf // 2):
+        copy.start()
+    load_u(0).start()
     for t in range(bits + 1):
         pl.semaphore_wait(ready.at[t], 1)
 
@@ -287,8 +410,9 @@
         size = (s.chips >> (t + 1)) * mb
         send_at.append((at, size))
         at += size
-    sz = gbuf.at[0, pl.ds(at, mb), pl.ds(0, ch)]
-    assert at + mb <= nbf
+    sz_at = at
+    sz = gbuf.at[0, pl.ds(sz_at, mb), pl.ds(0, ch)]
+    assert sz_at + mb <= nbf
     recvs = [r0] + [r1[t] for t in range(bits - 1)]
 
     def cols(n):
@@ -319,29 +443,30 @@
             pairs.append((base + mine * weight, base + (1 - mine) * weight))
         return pairs
 
+    def held(n, t, p, block):
+        rws, lane = rows_at(block * mb, mb, 128), pl.ds(p * 128, 128)
+        arrived = dt if t == 0 else recvs[t - 1]
+        mine = keep if t == 0 else ks[t - 1]
+        return mine[rws, lane] + arrived[rws, rows_at(n * ch + p * 128, 128, 128)].astype(F32)
+
     def halve(n, t):
-        held = keep if t == 0 else ks[t - 1]
         at, _ = send_at[t]
-
         for p in range(bits):
             lane = pl.ds(p * 128, 128)
 
             @pl.when(n >= 1)
             def _():
                 halve_copy(n - 1, t, p).wait_send()
-            for e, (kept, sent) in enumerate(blocks(t, p)):
-                gbuf[0, pl.ds(at + e * mb, mb), lane] = held[rows_at(sent * mb, mb, 128), lane].astype(BF16)
+            for e, (_, sent) in enumerate(blocks(t, p)):
+                gbuf[0, pl.ds(at + e * mb, mb), lane] = held(n, t, p, sent).astype(BF16)
             halve_copy(n, t, p).start()
-            for e, (kept, sent) in enumerate(blocks(t, p)):
-                ks[t][pl.ds(e * mb, mb), lane] = held[rows_at(kept * mb, mb, 128), lane]
+        for p in range(bits):
+            for e, (kept, _) in enumerate(blocks(t, p)):
+                ks[t][pl.ds(e * mb, mb), pl.ds(p * 128, 128)] = held(n, t, p, kept)
 
     def take(n, t):
-        _, size = send_at[t]
         for p in range(bits):
             halve_copy(n, t, p).wait_recv()
-            lane = pl.ds(p * 128, 128)
-            ks[t][pl.ds(0, size), lane] += recvs[t][
-                pl.ds(0, size), rows_at(n * ch + p * 128, 128, 128)].astype(F32)
 
     def plane_copy(n):
         shift = n // s.per_plane + 1
@@ -359,7 +484,8 @@
             @pl.when(n >= 1)
             def _():
                 plane_copy(n - 1).wait_send()
-            sz[...] = total[pl.ds(0, mb), :].astype(BF16)
+            for p in range(bits):
+                gbuf[0, pl.ds(sz_at, mb), pl.ds(p * 128, 128)] = held(n, bits, p, 0).astype(BF16)
             plane_copy(n).start()
 
         @pl.when(n >= away)
@@ -367,37 +493,38 @@
             c = n - away
             for t in range(s.n_gy - 1):
                 plane_copy(t * s.per_plane + c).wait_recv()
-                total[pl.ds(0, mb), :] += rz[pl.ds(t * mb, mb), cols(c)].astype(F32)
+            for p in range(bits):
+                block = held(n, bits, p, 0)
+                for t in range(s.n_gy - 1):
+                    block += rz[pl.ds(t * mb, mb), rows_at(c * ch + p * 128, 128, 128)].astype(F32)
+                total[pl.ds(0, mb), pl.ds(p * 128, 128)] = block
             copy = pltpu.make_async_copy(total.at[pl.ds(0, mb)], out.at[:, cols(c)], sem_l.at[0])
             copy.start()
             copy.wait()
 
-    core = bit[0]
-
     def b_step(n, carry):
         @pl.when(n < s.chunks)
         def _():
-            for part in range(2):
-                for copy in gu_copies(n, part):
-                    copy.wait()
-
-                def u_step(t, carry):
-                    rws = rows_at(t * s.pt, s.pt, 128)
-                    piece = lax.dot_general(
-                        w[rws, pl.ds(part * s.k_half, s.k_half)],
-                        dt[pl.ds(nbf // 2 + part * ch, ch), pl.ds(0, s.k_half)],
-                        (((1,), (1,)), ((), ())), preferred_element_type=F32)
-                    if part == 0:
-                        uf[rws, :] = piece
-                    else:
-                        gbuf[1, rws, pl.ds(0, ch)] = (uf[rws, :] + piece).astype(BF16)
-                    return carry
-                lax.fori_loop(0, tiles, u_step, 0)
-
-                @pl.when(n + 1 < s.chunks)
-                def _():
-                    for copy in gu_copies(n + 1, part):
-                        copy.start()
+            slot = lax.rem(n, 2)
+            for copy in gu_copies(n, 1, slot, dt, nbf // 2):
+                copy.wait()
+
+            @pl.when(n + 1 < s.chunks)
+            def _():
+                for copy in gu_copies(n + 1, 1, 1 - slot, dt, nbf // 2):
+                    copy.start()
+            load_u(n).wait()
+
+            def u_step(t, carry):
+                rws = rows_at(t * s.pt, s.pt, 128)
+                gbuf[1, rws, pl.ds(0, ch)] = (
+                    uf[rws, :] + u_product(n, t, 1, dt, nbf // 2)).astype(BF16)
+                return carry
+            lax.fori_loop(0, tiles, u_step, 0)
+
+            @pl.when(n + 1 < s.chunks)
+            def _():
+                load_u(n + 1).start()
 
         for t in reversed(range(bits)):
             m = n - 2 - t
@@ -413,25 +540,28 @@
         @pl.when(jnp.logical_and(n >= 1, n <= s.chunks))
         def _():
             swap_copy(n - 1).wait()
-            keep[...] += dt[pl.ds(0, half_rows), cols(n - 1)].astype(F32)
             halve(n - 1, 0)
 
         @pl.when(n < s.chunks)
         def _():
             def t_block(q, side):
-                return jnp.dot(coll_v[rows_at((2 * q + side) * mb, mb, 128), :],
+                if s.sorted_rows:
+                    at = side * half_rows + q * s.tt
+                else:
+                    at = (2 * q + (1 - core if side == 0 else core)) * mb
+                return jnp.dot(coll_v[rows_at(at, s.tt, 64), :],
                                gbuf[1, pl.ds(0, s.rows), pl.ds(0, ch)], preferred_element_type=F32)
 
             def sent(q, carry):
-                gbuf[0, rows_at(q * mb, mb, 128), pl.ds(0, ch)] = t_block(q, 1 - core).astype(BF16)
+                gbuf[0, rows_at(q * s.tt, s.tt, 64), pl.ds(0, ch)] = t_block(q, 0).astype(BF16)
                 return carry
-            lax.fori_loop(0, s.chips, sent, 0)
+            lax.fori_loop(0, half_rows // s.tt, sent, 0)
             swap_copy(n).start()
 
             def kept(q, carry):
-                keep[rows_at(q * mb, mb, 128), :] = t_block(q, core)
+                keep[rows_at(q * s.tt, s.tt, 64), :] = t_block(q, 1)
                 return carry
-            lax.fori_loop(0, s.chips, kept, 0)
+            lax.fori_loop(0, half_rows // s.tt, kept, 0)
         return carry
     lax.fori_loop(0, s.chunks + bits + 1, b_step, 0)
 
@@ -439,8 +569,10 @@
     for t in range(bits):
         for p in range(bits):
             halve_copy(s.chunks - 1, t, p).wait_send()
+    z_sends(lambda copy: copy.wait_send())
     for t in range(1, s.n_gy):
-        z_copy(t).wait_send()
+        for p in range(bits):
+            z_relays(t, p, lambda copy: copy.wait_send())
     for r in range(1, s.n_gx):
         for p in range(bits):
             for t in range(1, s.n_gy):
@@ -465,9 +597,10 @@
                 jax.ShapeDtypeStruct((s.mb, s.plane), F32),
                 jax.ShapeDtypeStruct((nbf, nbf), BF16),
                 jax.ShapeDtypeStruct((n_gx * s.halves, nbf, s.cw), BF16),
+                jax.ShapeDtypeStruct((s.chunks, rows, s.ch), F32),
             ),
             in_specs=[any_spec] * 3,
-            out_specs=(any_spec,) * 3,
+            out_specs=(any_spec,) * 4,
             scratch_shapes=[
                 pltpu.VMEM((nbf, rows), BF16),
                 pltpu.VMEM((s.t_rows, nbf), BF16),
@@ -481,8 +614,9 @@
                 pltpu.VMEM((nbf // 2, s.ch), F32),
                 ks,
                 pltpu.VMEM((rows, s.ch), F32),
-                dma((n_gy,)),
-                dma((n_gy,)),
+                dma((rows // s.pt,)),
+                dma((n_gy, s.bits)),
+                dma((2 * n_gy, s.bits)),
                 dma((n_gy, s.bits, n_gx)),
                 dma((n_gy, s.bits, n_gx)),
                 dma((s.halves, s.bits, n_gx)),
@@ -496,6 +630,8 @@
                 dma((s.bits, s.bits)),
                 dma((s.chunks,)),
                 dma((1,)),
+                dma((n_gx,)),
+                dma((n_gx,)),
                 pltpu.SemaphoreType.REGULAR((s.bits + 1,)),
             ],
             compiler_params=pltpu.CompilerParams(

time: 382 us -> 337 us (0.88)
  Pallas kernels: 379 us -> 333 us
    pallas_call x1, Pallas kernels: 379 us -> 333 us  [local(): pl.pallas_call(functools.partial(kernel_body, s), out_shape=(jax.ShapeDty...]
where the time goes in v2:
time: 337 us; the launch traced here: 335 us
  Pallas kernels  333 us (99%)
    pallas_call x1, Pallas kernels, local(): pl.pallas_call(functools.partial(kernel_body, s), out_shape=(jax.ShapeDty...  333 us

profile of v2, /device:TPU:18, one launch (start us, length us, event | category | flops | bytes accessed | tf_op | source)
XLA Modules:
  0.0 335.3 jit_solution(9719317991164852434)
XLA Ops:
  0.0 333.0 %exchange.1 = (f32[384,768]{1,0:T(8,128)}, bf16[3072,3072]{1,0:T(8,128)(2,1)}, bf16[16,3072,256]{2,1,0:T(8,128)(2,1)}, f32[12,2048,256]{2,1,0:T(8,128)}) custom-call(bf16[3072,2048]{1,0:T(8,128)(2,1)} %coll.1, bf16[768,3072]{1,0:T(8,128)(2,1)} %dens.1, bf16[2048,8,512]{2,1,0:T(8,128)(2,1)} %bitcast.1), custom_call_target="tpu_custom_call" | custom-call | tf_op jit(solution)/shard_map/exchange/pallas_call | solution.py:594
  333.0 2.4 copy.5
